TPU v7x, 512 devices: a whole 4x8x8 slice. The times are simulated.
512 devices in a mesh: fsdp: 64 (over x, y, core), dp: 8 (over z).
Axes of the slice: x: 4, y: 8, z: 8, core: 2. Of those that a mesh axis runs over, the one named last changes fastest.
Arguments:
- grads: bfloat16 [8, 1024, 28672], P('dp', 'fsdp')
- block_slot: int32 [28], replicated, may hold values from 0 to 63, as said below
- left_stats: float32 [64, 1024, 1024], P('fsdp', 'dp')
- right_stats: float32 [64, 1024, 1024], P('fsdp', 'dp')
- left_root: bfloat16 [64, 1024, 1024], P('fsdp', 'dp')
- right_root: bfloat16 [64, 1024, 1024], P('fsdp', 'dp')
Outputs:
- left_new: float32 [64, 1024, 1024], P('fsdp', 'dp')
- right_new: float32 [64, 1024, 1024], P('fsdp', 'dp')
- update: bfloat16 [1024, 28672], P('fsdp')
Inputs may be any that keep to these rules, and one draw needn't show every extreme that they name: The entries of block_slot are distinct. Block b's statistics and roots sit in slot block_slot[b], which belongs to the fsdp device of index block_slot[b]; slots that no block names are empty and their statistics pass through unchanged.
All inputs are finite; a program needn't handle non-finite values.
Results may differ from a plain program's by a relative error of at most 0.015.
Values may be sent and summed in bfloat16 or wider, within the bound.
No kernel may reach another device: no remote copies, remote signals or barrier semaphores. Data moves between devices by JAX's collectives and lax.ppermute only.
A program may use at most 64 MiB of HBM per device.

v0:
```python
import jax
import jax.numpy as jnp
from jax import lax
from jax.sharding import Mesh
from jax.sharding import PartitionSpec as P

FSDP = ("fsdp_0", "fsdp_1", "fsdp_2")
epsilon = 1e-06


def split_terms(value):
    high = lax.reduce_precision(value, 8, 7)
    middle = lax.reduce_precision(value - high, 8, 7)
    low = value - high - middle
    return [term.astype(jnp.bfloat16) for term in (high, middle, low)]


def per_device(grads, block_slot, left_stats, right_stats, left_root, right_root):
    rows = grads[0]
    row_dev, col_count = rows.shape
    block_size = left_stats.shape[2]
    block_count = col_count // block_size
    shared = left_stats.shape[1]
    replicas = lax.axis_size("dp")
    total_slots = lax.axis_size(FSDP)
    slot_ids = jnp.arange(total_slots, dtype=jnp.int32)
    matches = block_slot[None, :] == slot_ids[:, None]
    filled = jnp.any(matches, axis=1)
    numbers = jnp.arange(block_count, dtype=jnp.int32)
    source = jnp.sum(jnp.where(matches, numbers[None, :], 0), axis=1)
    whole_left = lax.all_gather(left_root[0], "dp", axis=0, tiled=True)
    shares = rows.reshape(row_dev, block_count, replicas, shared).transpose(2, 1, 0, 3)
    shares = shares.reshape(replicas, block_count * row_dev, shared)
    roots = right_root[0].reshape(shared, replicas, shared).transpose(1, 0, 2)
    message = jnp.concatenate([shares, roots], axis=1)
    received = lax.all_to_all(message, "dp", 0, 0, tiled=True)
    summed = jnp.sum(received[:, : block_count * row_dev].astype(jnp.float32), axis=0)
    summed = summed.astype(jnp.bfloat16).reshape(block_count, row_dev, shared)
    right_cols = received[:, block_count * row_dev :]
    outgoing = jnp.where(
        filled[:, None, None], jnp.take(summed, source, axis=0), jnp.zeros((), jnp.bfloat16)
    )
    incoming = lax.all_to_all(outgoing, FSDP, 0, 0, tiled=True)
    mine, whole_left = lax.optimization_barrier((incoming.reshape(block_size, shared), whole_left))
    gradient = lax.all_gather(mine, "dp", axis=1, tiled=True)
    inner = jnp.einsum(
        "rk,kc->rc",
        gradient,
        right_cols.reshape(block_size, shared),
        preferred_element_type=jnp.float32,
    )
    high = lax.reduce_precision(inner, 8, 7)
    low = (inner - high).astype(jnp.bfloat16)
    high = high.astype(jnp.bfloat16)
    both = jnp.einsum(
        "kr,rc->kc", whole_left, high, preferred_element_type=jnp.float32
    ) + jnp.einsum("kr,rc->kc", whole_left, low, preferred_element_type=jnp.float32)
    partial = split_terms(jnp.sum(both * both))
    lanes = jnp.concatenate([jnp.stack(partial), jnp.zeros(shared - 3, jnp.bfloat16)])
    marks = jnp.broadcast_to(lanes[None, None, :], (total_slots, 8, shared))
    both = both.astype(jnp.bfloat16).reshape(total_slots, row_dev, shared)
    back = lax.all_to_all(jnp.concatenate([both, marks], axis=1), FSDP, 0, 0, tiled=True)
    row_start = lax.axis_index("dp") * shared
    own_rows = lax.dynamic_slice_in_dim(gradient, row_start, shared, 0)
    left_new = left_stats + jnp.einsum(
        "rc,kc->rk", own_rows, gradient, preferred_element_type=jnp.float32
    )
    right_new = right_stats + jnp.einsum(
        "rc,rk->ck", mine, gradient, preferred_element_type=jnp.float32
    )
    picked = jnp.take(back, block_slot, axis=0)
    terms = jnp.zeros((32, shared), jnp.bfloat16).at[:block_count].set(picked[:, row_dev, :])
    tiles = picked[:, :row_dev].reshape(block_count * row_dev, shared)
    gathered = lax.all_gather(jnp.concatenate([tiles, terms]), "dp", axis=0, tiled=False)
    full = gathered[:, : block_count * row_dev].reshape(replicas, block_count, row_dev, shared)
    terms = gathered[:, block_count * row_dev :][:, :block_count, :3].astype(jnp.float32)
    squares = jnp.sum(terms, axis=(0, 2))
    factor = lax.rsqrt(squares / (block_size * block_size) + epsilon)
    update = (full.astype(jnp.float32) * factor[None, :, None, None]).astype(jnp.bfloat16)
    update = update.transpose(2, 1, 0, 3).reshape(row_dev, col_count)
    return (left_new, right_new, update)


def solution(mesh):
    split = Mesh(
        mesh.devices.reshape(4, 8, 2, mesh.shape["dp"]), ("fsdp_0", "fsdp_1", "fsdp_2", "dp")
    )
    placed = (
        P("dp", FSDP, None),
        P(),
        P(FSDP, "dp", None),
        P(FSDP, "dp", None),
        P(FSDP, "dp", None),
        P(FSDP, "dp", None),
    )
    return jax.shard_map(
        per_device,
        mesh=split,
        in_specs=placed,
        out_specs=(P(FSDP, "dp", None), P(FSDP, "dp", None), P(FSDP, None)),
        check_vma=False,
    )
```

profile of v0, /device:TPU:8, one launch (start us, length us, event | category | flops | bytes accessed | tf_op | source)
XLA Modules:
  0.0 203.1 jit_solution(17511728519001342608)
XLA Ops:
  7.2 0.0 all-gather.7.cloned.1.call-start
  7.2 0.7 all-gather.7.cloned.1.call-update
  7.9 1.1 copy.15
  9.0 0.2 copy.16
  9.2 1.3 copy.19
  10.5 0.4 copy.14
  10.9 0.0 copy-start.6
  10.9 1.1 pad_maximum_fusion
  12.0 10.3 %all-to-all-start = ((bf16[8,576,128]{2,1,0:T(8,128)(2,1)}), bf16[8,576,128]{2,1,0:T(8,128)(2,1)S(1)}, u32[]{:S(2)}, u32[]{:S(2)}) async-start(bf16[8,576,128]{2,1,0:T(8,128)(2,1)} %pad_maximum_fusion), calls=%async_computation | async-start | bytes 2359296 | tf_op jit(solution)/shard_map/all_to_all | solution.py:36
  22.3 0.0 all-gather.5.cloned.1.call-start
  22.4 0.0 copy-done.6
  22.4 0.1 select_reduce_fusion
  22.5 0.1 fusion.10
  22.6 42.0 %all-to-all-done = bf16[8,576,128]{2,1,0:T(8,128)(2,1)S(1)} async-done(((bf16[8,576,128]{2,1,0:T(8,128)(2,1)}), bf16[8,576,128]{2,1,0:T(8,128)(2,1)S(1)}, u32[]{:S(2)}, u32[]{:S(2)}) %all-to-all-start) | async-done | bytes 1179680 | tf_op jit(solution)/shard_map/all_to_all | solution.py:36
  64.5 0.1 slice_reduce_fusion
  64.7 0.6 gather_fusion
  65.3 0.2 select_select_fusion
  65.5 22.5 %all_to_all.15 = bf16[64,16,128]{2,1,0:T(8,128)(2,1)} all-to-all(bf16[64,16,128]{2,1,0:T(8,128)(2,1)S(1)} %select_select_fusion), channel_id=1, replica_groups=mesh['fsdp_0'=4,'fsdp_1'=8,'fsdp_2'=2,'dp'=8] {'fsdp_0','fsdp_1','fsdp_2'}, dimensions={0} | all-to-all | bytes 524288 | tf_op jit(solution)/shard_map/all_to_all | solution.py:43
  88.0 0.0 all-gather.7.cloned.1.call-done
  88.0 0.0 copy-start.1
  88.0 0.0 all-gather.5.cloned.1.call-update
  88.0 42.6 %all-gather.5.cloned.1.call-done = bf16[1024,1024]{1,0:T(8,128)(2,1)} async-done(((bf16[1024,128]{1,0:T(8,128)(2,1)}), bf16[1024,1024]{1,0:T(8,128)(2,1)}) %all-gather.5.cloned.1.call-update) | async-done | bytes 2097168 | tf_op jit(solution)/shard_map/all_gather | solution.py:45
  130.7 2.3 %fusion.14 = f32[1024,128]{1,0:T(8,128)S(1)} fusion(bf16[1024,1024]{1,0:T(8,128)(2,1)} %all-gather.5.cloned.1.call-done, bf16[1024,128]{1,0:T(8,128)(2,1)S(1)} %bitcast.64), kind=kOutput, calls=%fused_computation.42 | convolution fusion | flops 268435456 | bytes 2883584 | tf_op jit(solution)/shard_map/rk,kc->rc/dot_general | solution.py:46
  133.0 0.0 copy-done.1
  133.0 0.0 copy-start.2
  133.0 0.7 fusion.6
  133.7 0.9 copy-done.2
  134.6 0.0 copy-start
  134.6 1.3 fusion.13
  140.8 0.1 pad_maximum_fusion.2
  140.9 0.8 pad_maximum_fusion.1
  141.7 10.4 %all-to-all-start.2 = ((bf16[64,24,128]{2,1,0:T(8,128)(2,1)}), bf16[64,24,128]{2,1,0:T(8,128)(2,1)S(1)}, u32[]{:S(2)}, u32[]{:S(2)}) async-start(bf16[64,24,128]{2,1,0:T(8,128)(2,1)} %pad_maximum_fusion.1), calls=%async_computation.2 | async-start | bytes 786432 | tf_op jit(solution)/shard_map/all_to_all | solution.py:62
  152.1 0.0 copy-start.5
  152.1 0.0 copy-done
  152.2 0.0 copy-done.4
  152.2 1.6 fusion.1
  153.8 0.0 copy-done.3
  153.8 0.0 copy-done.5
  153.8 1.3 fusion.2
  155.1 11.5 %all-to-all-done.2 = bf16[64,24,128]{2,1,0:T(8,128)(2,1)S(1)} async-done(((bf16[64,24,128]{2,1,0:T(8,128)(2,1)}), bf16[64,24,128]{2,1,0:T(8,128)(2,1)S(1)}, u32[]{:S(2)}, u32[]{:S(2)}) %all-to-all-start.2) | async-done | bytes 393248 | tf_op jit(solution)/shard_map/all_to_all | solution.py:62
  166.5 0.6 gather_fusion.1
  167.1 0.1 broadcast_select_fusion
  167.3 26.6 %all-gather.1 = bf16[3840,128]{1,0:T(8,128)(2,1)S(1)} all-gather(bf16[480,128]{1,0:T(8,128)(2,1)S(1)} %fusion.9), channel_id=3, replica_groups=mesh['fsdp_0'=4,'fsdp_1'=8,'fsdp_2'=2,'dp'=8] {'dp'}, dimensions={0}, use_global_device_ids=true | all-gather | bytes 1105920 | tf_op jit(solution)/shard_map/all_gather | solution.py:74
  193.9 0.1 convert_reduce_fusion
  194.1 0.1 slice.50
  194.2 0.3 fusion.3
  194.4 0.6 copy.17
  195.0 1.3 copy.23
  (16 shorter events, 0.1 us)
Async XLA Ops:
  7.2 80.8 %all-gather.7.cloned.1.call-start = ((), (), s32[]{:S(2)}) async-start(), calls=%async_computation.4 | async-start | bytes 2359296 | tf_op jit(solution)/shard_map/all_gather | solution.py:31
  10.9 11.5 %copy-start.6 = (s32[28]{0:T(128)S(1)}, s32[28]{0:T(128)}, u32[]{:S(2)}) copy-start(s32[28]{0:T(128)} %param.9) | copy-start | bytes 340
  12.0 52.5 %all-to-all-start = ((bf16[8,576,128]{2,1,0:T(8,128)(2,1)}), bf16[8,576,128]{2,1,0:T(8,128)(2,1)S(1)}, u32[]{:S(2)}, u32[]{:S(2)}) async-start(bf16[8,576,128]{2,1,0:T(8,128)(2,1)} %pad_maximum_fusion), calls=%async_computation | async-start | bytes 2359296 | tf_op jit(solution)/shard_map/all_to_all | solution.py:36
  22.3 108.3 %all-gather.5.cloned.1.call-start = ((), (), s32[]{:S(2)}) async-start(), calls=%async_computation.3 | async-start | bytes 2359296 | tf_op jit(solution)/shard_map/all_gather | solution.py:45
  88.0 45.0 %copy-start.1 = (bf16[1,1024,1024]{2,1,0:T(8,128)(2,1)S(1)}, bf16[1,1024,1024]{2,1,0:T(8,128)(2,1)}, u32[]{:S(2)}) copy-start(bf16[1,1024,1024]{2,1,0:T(8,128)(2,1)} %all-gather.7.cloned.1.call-done) | copy-start | bytes 6291460
  133.0 1.6 copy-start.2
  134.6 17.6 %copy-start = (bf16[1024,1024]{1,0:T(8,128)(2,1)S(1)}, bf16[1024,1024]{1,0:T(8,128)(2,1)}, u32[]{:S(2)}) copy-start(bf16[1024,1024]{1,0:T(8,128)(2,1)} %all-gather.5.cloned.1.call-done) | copy-start | bytes 6291460
  134.6 17.6 %copy-start.4 = (f32[1,128,1024]{2,1,0:T(8,128)S(1)}, f32[1,128,1024]{2,1,0:T(8,128)}, u32[]{:S(2)}) copy-start(f32[1,128,1024]{2,1,0:T(8,128)} %param.10) | copy-start | bytes 1572868
  141.7 12.1 %copy-start.3 = (bf16[64,16,128]{2,1,0:T(8,128)(2,1)S(1)}, bf16[64,16,128]{2,1,0:T(8,128)(2,1)}, u32[]{:S(2)}) copy-start(bf16[64,16,128]{2,1,0:T(8,128)(2,1)} %all_to_all.15) | copy-start | bytes 786436
  141.7 24.8 %all-to-all-start.2 = ((bf16[64,24,128]{2,1,0:T(8,128)(2,1)}), bf16[64,24,128]{2,1,0:T(8,128)(2,1)S(1)}, u32[]{:S(2)}, u32[]{:S(2)}) async-start(bf16[64,24,128]{2,1,0:T(8,128)(2,1)} %pad_maximum_fusion.1), calls=%async_computation.2 | async-start | bytes 786432 | tf_op jit(solution)/shard_map/all_to_all | solution.py:62
  152.1 1.7 copy-start.5
Sparse Core Ops, SparseCore 0:
  10.1 64.5 all-gather.6
  88.1 42.4 all-gather.4
where the time goes:
time: 204 us; the launch traced here: 203 us
  waiting for transfers between devices  96.7 us (47%)
  blocking collectives  49.1 us (24%)
  starting transfers between devices  20.8 us (10%)
  between operations  19.2 us (9%)
  matrix products  7.21 us (4%)
  local copies, waits for them, and re-layouts  7.09 us (3%)
  other arithmetic  3.03 us (1%)
    all_gather x1, waiting for transfers between devices, per_device(): gradient = lax.all_gather(mine, 'dp', axis=1, tiled=True)  42.6 us
    all_to_all x1, waiting for transfers between devices, per_device(): received = lax.all_to_all(message, 'dp', 0, 0, tiled=True)  42 us
    all_gather x1, blocking collectives, per_device(): lax.all_gather(jnp.concatenate([tiles, terms]), 'dp', axis=0, tiled=False)  26.6 us
    all_to_all x1, blocking collectives, per_device(): incoming = lax.all_to_all(outgoing, FSDP, 0, 0, tiled=True)  22.5 us
    all_to_all x1, waiting for transfers between devices, per_device(): lax.all_to_all(jnp.concatenate([both, marks], axis=1), FSDP, 0, 0, tiled=...  11.5 us
    all_to_all x1, starting transfers between devices, per_device(): lax.all_to_all(jnp.concatenate([both, marks], axis=1), FSDP, 0, 0, tiled=...  10.4 us
    all_to_all x1, starting transfers between devices, per_device(): received = lax.all_to_all(message, 'dp', 0, 0, tiled=True)  10.3 us
    unnamed x18, local copies, waits for them, and re-layouts  4.61 us
  transfers between devices with their start and end apart: 4, of which 3 were waited for; matrix products, arithmetic and copies ran while one was open for 4% of the time, Pallas kernels for 0%

commit v1 on v0

--- a/solution.py
+++ b/solution.py
@@ -6,6 +6,12 @@
 
 FSDP = ("fsdp_0", "fsdp_1", "fsdp_2")
 epsilon = 1e-06
+
+
+def gather_by_exchange(x, axis, dim):
+    count = lax.axis_size(axis)
+    repeats = [count if d == dim else 1 for d in range(x.ndim)]
+    return lax.all_to_all(jnp.tile(x, repeats), axis, split_axis=dim, concat_axis=dim, tiled=True)
 
 
 def split_terms(value):
@@ -42,7 +48,7 @@
     )
     incoming = lax.all_to_all(outgoing, FSDP, 0, 0, tiled=True)
     mine, whole_left = lax.optimization_barrier((incoming.reshape(block_size, shared), whole_left))
-    gradient = lax.all_gather(mine, "dp", axis=1, tiled=True)
+    gradient = gather_by_exchange(mine, "dp", 1)
     inner = jnp.einsum(
         "rk,kc->rc",
         gradient,

time: 204 us -> 210 us (1.029)
  waiting for transfers between devices: 96.7 us -> 100 us
  local copies, waits for them, and re-layouts: 7.09 us -> 10.3 us
    all_to_all x0 -> x1, waiting for transfers between devices: none -> 51.8 us  [gather_by_exchange(): lax.all_to_all(jnp.tile(x, repeats), axis, split_axis=dim, concat_axis=di...]
    all_gather x1 -> x0, waiting for transfers between devices: 42.6 us -> none  [per_device(): gradient = lax.all_gather(mine, 'dp', axis=1, tiled=True)]
    all_to_all x1, waiting for transfers between devices: 11.5 us -> 7.02 us  [per_device(): lax.all_to_all(jnp.concatenate([both, marks], axis=1), FSDP, 0, 0, tiled=...]
    all_to_all x1, starting transfers between devices: 10.4 us -> 6.03 us  [per_device(): lax.all_to_all(jnp.concatenate([both, marks], axis=1), FSDP, 0, 0, tiled=...]
    all_to_all x0 -> x1, starting transfers between devices: none -> 3.6 us  [gather_by_exchange(): lax.all_to_all(jnp.tile(x, repeats), axis, split_axis=dim, concat_axis=di...]
    all_to_all x0 -> x1, local copies, waits for them, and re-layouts: none -> 2.61 us  [gather_by_exchange(): lax.all_to_all(jnp.tile(x, repeats), axis, split_axis=dim, concat_axis=di...]
    unnamed x18 -> x16, local copies, waits for them, and re-layouts: 4.61 us -> 3.66 us
  transfers between devices with their start and end apart: 4 -> 4, of which waited for: 3 -> 3; matrix products, arithmetic and copies ran while one was open for 4% -> 6% of each run, Pallas kernels for 0% -> 0%
where the time goes in v1:
time: 210 us; the launch traced here: 209 us
  waiting for transfers between devices  100 us (48%)
  blocking collectives  49 us (23%)
  starting transfers between devices  20 us (10%)
  between operations  19.2 us (9%)
  local copies, waits for them, and re-layouts  10.3 us (5%)
  matrix products  7.46 us (4%)
  other arithmetic  3.03 us (1%)
    all_to_all x1, waiting for transfers between devices, gather_by_exchange(): lax.all_to_all(jnp.tile(x, repeats), axis, split_axis=dim, concat_axis=di...  51.8 us
    all_to_all x1, waiting for transfers between devices, per_device(): received = lax.all_to_all(message, 'dp', 0, 0, tiled=True)  41 us
    all_gather x1, blocking collectives, per_device(): lax.all_gather(jnp.concatenate([tiles, terms]), 'dp', axis=0, tiled=False)  26.6 us
    all_to_all x1, blocking collectives, per_device(): incoming = lax.all_to_all(outgoing, FSDP, 0, 0, tiled=True)  22.4 us
    all_to_all x1, starting transfers between devices, per_device(): received = lax.all_to_all(message, 'dp', 0, 0, tiled=True)  10.3 us
    all_to_all x1, waiting for transfers between devices, per_device(): lax.all_to_all(jnp.concatenate([both, marks], axis=1), FSDP, 0, 0, tiled=...  7.02 us
    all_to_all x1, starting transfers between devices, per_device(): lax.all_to_all(jnp.concatenate([both, marks], axis=1), FSDP, 0, 0, tiled=...  6.03 us
  transfers between devices with their start and end apart: 4, of which 3 were waited for; matrix products, arithmetic and copies ran while one was open for 6% of the time, Pallas kernels for 0%

profile of v1, /device:TPU:8, one launch (start us, length us, event | category | flops | bytes accessed | tf_op | source)
XLA Modules:
  0.0 209.4 jit_solution(18382089865148208705)
XLA Ops:
  7.2 0.0 copy-start.4
  7.2 0.0 all-gather.4.cloned.1.call-start
  7.2 0.7 all-gather.4.cloned.1.call-update
  7.9 1.3 copy.25
  9.2 0.4 copy.19
  9.6 0.0 copy-done.4
  9.6 0.2 copy.20
  9.8 0.2 copy.21
  9.9 0.0 copy-start.5
  10.0 1.1 pad_maximum_fusion
  11.1 10.3 %all-to-all-start = ((bf16[8,576,128]{2,1,0:T(8,128)(2,1)}), bf16[8,576,128]{2,1,0:T(8,128)(2,1)S(1)}, u32[]{:S(2)}, u32[]{:S(2)}) async-start(bf16[8,576,128]{2,1,0:T(8,128)(2,1)} %pad_maximum_fusion), calls=%async_computation | async-start | bytes 2359296 | tf_op jit(solution)/shard_map/all_to_all | solution.py:42
  21.4 0.0 copy-done.5
  21.4 0.1 select_reduce_fusion
  21.5 0.1 fusion.11
  21.6 41.0 %all-to-all-done = bf16[8,576,128]{2,1,0:T(8,128)(2,1)S(1)} async-done(((bf16[8,576,128]{2,1,0:T(8,128)(2,1)}), bf16[8,576,128]{2,1,0:T(8,128)(2,1)S(1)}, u32[]{:S(2)}, u32[]{:S(2)}) %all-to-all-start) | async-done | bytes 1179680 | tf_op jit(solution)/shard_map/all_to_all | solution.py:42
  62.6 0.1 slice_reduce_fusion
  62.7 0.6 gather_fusion
  63.3 0.2 select_select_fusion
  63.5 22.4 %all_to_all.24 = bf16[64,16,128]{2,1,0:T(8,128)(2,1)S(1)} all-to-all(bf16[64,16,128]{2,1,0:T(8,128)(2,1)S(1)} %select_select_fusion), channel_id=1, replica_groups=mesh['fsdp_0'=4,'fsdp_1'=8,'fsdp_2'=2,'dp'=8] {'fsdp_0','fsdp_1','fsdp_2'}, dimensions={0} | all-to-all | bytes 524288 | tf_op jit(solution)/shard_map/all_to_all | solution.py:49
  85.9 0.0 all-gather.4.cloned.1.call-done
  85.9 1.6 tile.2
  87.5 3.6 %all-to-all-start.2 = ((bf16[1024,8,128]{2,0,1:T(8,128)(2,1)}), bf16[1024,8,128]{2,0,1:T(8,128)(2,1)S(1)}, u32[]{:S(2)}, u32[]{:S(2)}) async-start(bf16[1024,8,128]{2,0,1:T(8,128)(2,1)} %tile.2), calls=%async_computation.2 | async-start | bytes 4194304 | tf_op jit(solution)/shard_map/all_to_all | solution.py:14
  91.1 51.8 %all-to-all-done.2 = bf16[1024,8,128]{2,0,1:T(8,128)(2,1)S(1)} async-done(((bf16[1024,8,128]{2,0,1:T(8,128)(2,1)}), bf16[1024,8,128]{2,0,1:T(8,128)(2,1)S(1)}, u32[]{:S(2)}, u32[]{:S(2)}) %all-to-all-start.2) | async-done | bytes 2097184 | tf_op jit(solution)/shard_map/all_to_all | solution.py:14
  142.8 0.0 copy-start.1
  142.8 0.7 convolution_bitcast_fusion
  143.6 0.9 copy-done.1
  144.4 0.7 fusion.6
  145.1 1.3 fusion.14
  151.4 0.1 pad_maximum_fusion.2
  151.5 0.8 pad_maximum_fusion.1
  152.3 6.0 %all-to-all-start.3 = ((bf16[64,24,128]{2,1,0:T(8,128)(2,1)}), bf16[64,24,128]{2,1,0:T(8,128)(2,1)S(1)}, u32[]{:S(2)}, u32[]{:S(2)}) async-start(bf16[64,24,128]{2,1,0:T(8,128)(2,1)} %pad_maximum_fusion.1), calls=%async_computation.3 | async-start | bytes 786432 | tf_op jit(solution)/shard_map/all_to_all | solution.py:68
  158.4 0.0 copy-start.2
  158.4 2.6 %copy.22 = bf16[1024,8,128]{0,2,1:T(8,128)(2,1)} copy(bf16[1024,8,128]{2,0,1:T(8,128)(2,1)S(1)} %all-to-all-done.2) | data formatting | bytes 4194304 | tf_op jit(solution)/shard_map/all_to_all | solution.py:14
  161.0 0.0 copy-start
  161.0 0.0 copy-done.2
  161.0 3.1 %fusion.1 = f32[1,128,1024]{2,1,0:T(8,128)} fusion(f32[1,128,1024]{2,1,0:T(8,128)S(1)} %copy-done.2, bf16[1024,1024]{0,1:T(8,128)(2,1)} %bitcast.51, s32[]{:T(128)S(6)} %select_n.45), kind=kOutput, calls=%fused_computation.8 | convolution fusion | flops 268566528 | bytes 3407876 | tf_op jit(solution)/shard_map/rc,kc->rk/dot_general | solution.py:71
  164.1 0.0 copy-done
  164.1 0.0 copy-done.3
  164.1 1.6 fusion.2
  165.7 7.0 %all-to-all-done.3 = bf16[64,24,128]{2,1,0:T(8,128)(2,1)S(1)} async-done(((bf16[64,24,128]{2,1,0:T(8,128)(2,1)}), bf16[64,24,128]{2,1,0:T(8,128)(2,1)S(1)}, u32[]{:S(2)}, u32[]{:S(2)}) %all-to-all-start.3) | async-done | bytes 393248 | tf_op jit(solution)/shard_map/all_to_all | solution.py:68
  172.7 0.6 gather_fusion.1
  173.3 0.1 broadcast_select_fusion
  173.5 26.6 %all-gather.1 = bf16[3840,128]{1,0:T(8,128)(2,1)S(1)} all-gather(bf16[480,128]{1,0:T(8,128)(2,1)S(1)} %fusion.10), channel_id=3, replica_groups=mesh['fsdp_0'=4,'fsdp_1'=8,'fsdp_2'=2,'dp'=8] {'dp'}, dimensions={0}, use_global_device_ids=true | all-gather | bytes 1105920 | tf_op jit(solution)/shard_map/all_gather | solution.py:80
  200.2 0.1 slice.50
  200.2 0.1 convert_reduce_fusion
  200.4 0.3 fusion.3
  200.6 0.6 copy.23
  201.2 1.3 copy.29
  (14 shorter events, 0.1 us)
Async XLA Ops:
  7.2 2.4 %copy-start.4 = (bf16[1,128,1024]{2,1,0:T(8,128)(2,1)S(1)}, bf16[1,128,1024]{2,1,0:T(8,128)(2,1)}, u32[]{:S(2)}) copy-start(bf16[1,128,1024]{2,1,0:T(8,128)(2,1)} %param.13) | copy-start | bytes 786436
  7.2 78.7 %all-gather.4.cloned.1.call-start = ((), (), s32[]{:S(2)}) async-start(), calls=%async_computation.4 | async-start | bytes 2359296 | tf_op jit(solution)/shard_map/all_gather | solution.py:37
  9.9 11.4 %copy-start.5 = (s32[28]{0:T(128)S(1)}, s32[28]{0:T(128)}, u32[]{:S(2)}) copy-start(s32[28]{0:T(128)} %param.9) | copy-start | bytes 340
  11.1 51.5 %all-to-all-start = ((bf16[8,576,128]{2,1,0:T(8,128)(2,1)}), bf16[8,576,128]{2,1,0:T(8,128)(2,1)S(1)}, u32[]{:S(2)}, u32[]{:S(2)}) async-start(bf16[8,576,128]{2,1,0:T(8,128)(2,1)} %pad_maximum_fusion), calls=%async_computation | async-start | bytes 2359296 | tf_op jit(solution)/shard_map/all_to_all | solution.py:42
  87.5 55.4 %all-to-all-start.2 = ((bf16[1024,8,128]{2,0,1:T(8,128)(2,1)}), bf16[1024,8,128]{2,0,1:T(8,128)(2,1)S(1)}, u32[]{:S(2)}, u32[]{:S(2)}) async-start(bf16[1024,8,128]{2,0,1:T(8,128)(2,1)} %tile.2), calls=%async_computation.2 | async-start | bytes 4194304 | tf_op jit(solution)/shard_map/all_to_all | solution.py:14
  142.8 1.6 copy-start.1
  152.3 20.5 %all-to-all-start.3 = ((bf16[64,24,128]{2,1,0:T(8,128)(2,1)}), bf16[64,24,128]{2,1,0:T(8,128)(2,1)S(1)}, u32[]{:S(2)}, u32[]{:S(2)}) async-start(bf16[64,24,128]{2,1,0:T(8,128)(2,1)} %pad_maximum_fusion.1), calls=%async_computation.3 | async-start | bytes 786432 | tf_op jit(solution)/shard_map/all_to_all | solution.py:68
  158.4 2.6 %copy-start.2 = (f32[1,128,1024]{2,1,0:T(8,128)S(1)}, f32[1,128,1024]{2,1,0:T(8,128)}, u32[]{:S(2)}) copy-start(f32[1,128,1024]{2,1,0:T(8,128)} %param.10) | copy-start | bytes 1572868
  161.0 3.1 %copy-start = (bf16[1024,8,128]{0,2,1:T(8,128)(2,1)S(1)}, bf16[1024,8,128]{0,2,1:T(8,128)(2,1)}, u32[]{:S(2)}) copy-start(bf16[1024,8,128]{0,2,1:T(8,128)(2,1)} %copy.22) | copy-start | bytes 6291460
  161.0 3.1 %copy-start.3 = (f32[1,128,1024]{2,1,0:T(8,128)S(1)}, f32[1,128,1024]{2,1,0:T(8,128)}, u32[]{:S(2)}) copy-start(f32[1,128,1024]{2,1,0:T(8,128)} %param.11) | copy-start | bytes 1572868
Sparse Core Ops, SparseCore 0:
  10.1 63.5 all-gather.3
